TPU v7x, 32 devices: a whole 2x2x4 slice. The times are simulated.
32 devices in a mesh: job: 2 (over core), replica: 4 (over z), model: 4 (over y, x).
Axes of the slice: x: 2, y: 2, z: 4, core: 2. Of those that a mesh axis runs over, the one named last changes fastest.
Arguments:
- grad_query: float32 [8, 1024, 1024], P(('job', 'replica'), None, 'model'), parts along dimension 0, may hold values from -0.875 to 0.875
- grad_key: float32 [8, 1024, 1024], P(('job', 'replica'), None, 'model'), parts along dimension 0, may hold values from -0.875 to 0.875
- grad_value: float32 [8, 1024, 1024], P(('job', 'replica'), None, 'model'), parts along dimension 0, may hold values from -0.875 to 0.875
- grad_mixed: float32 [8, 1024, 1024], P(('job', 'replica'), 'model'), parts along dimension 0, may hold values from -0.875 to 0.875
- grad_norm: float32 [8, 1024], P(('job', 'replica')), parts along dimension 0, may hold values from -8 to 8
- weight_query: float32 [2048, 1024], P(('job', 'replica'), 'model'), parts along dimension 0, may hold values from -0.25 to 0.25
- weight_key: float32 [2048, 1024], P(('job', 'replica'), 'model'), parts along dimension 0, may hold values from -0.25 to 0.25
- weight_value: float32 [2048, 1024], P(('job', 'replica'), 'model'), parts along dimension 0, may hold values from -0.25 to 0.25
- weight_mixed: float32 [2048, 1024], P(('job', 'model'), 'replica'), parts along dimension 0, may hold values from -0.25 to 0.25
- weight_norm: float32 [2048], P(('job', 'replica')), parts along dimension 0, may hold values from 0.25 to 1.75
- moment_query: float32 [2048, 1024], P(('job', 'replica'), 'model'), parts along dimension 0, may hold values from -0.1875 to 0.1875
- moment_key: float32 [2048, 1024], P(('job', 'replica'), 'model'), parts along dimension 0, may hold values from -0.1875 to 0.1875
- moment_value: float32 [2048, 1024], P(('job', 'replica'), 'model'), parts along dimension 0, may hold values from -0.1875 to 0.1875
- moment_mixed: float32 [2048, 1024], P(('job', 'model'), 'replica'), parts along dimension 0, may hold values from -0.1875 to 0.1875
- moment_norm: float32 [2048], P(('job', 'replica')), parts along dimension 0, may hold values from -1.75 to 1.75
Outputs:
- copy_query: bfloat16 [2048, 1024], P('job', 'model'), parts along dimension 0
- copy_key: bfloat16 [2048, 1024], P('job', 'model'), parts along dimension 0
- copy_value: bfloat16 [2048, 1024], P('job', 'model'), parts along dimension 0
- copy_mixed: bfloat16 [2048, 1024], P(('job', 'model')), parts along dimension 0
- copy_norm: bfloat16 [2048], P('job'), parts along dimension 0
- new_query: float32 [2048, 1024], P(('job', 'replica'), 'model'), parts along dimension 0
- new_key: float32 [2048, 1024], P(('job', 'replica'), 'model'), parts along dimension 0
- new_value: float32 [2048, 1024], P(('job', 'replica'), 'model'), parts along dimension 0
- new_mixed: float32 [2048, 1024], P(('job', 'model'), 'replica'), parts along dimension 0
- new_norm: float32 [2048], P(('job', 'replica')), parts along dimension 0
- state_new_query: float32 [2048, 1024], P(('job', 'replica'), 'model'), parts along dimension 0
- state_new_key: float32 [2048, 1024], P(('job', 'replica'), 'model'), parts along dimension 0
- state_new_value: float32 [2048, 1024], P(('job', 'replica'), 'model'), parts along dimension 0
- state_new_mixed: float32 [2048, 1024], P(('job', 'model'), 'replica'), parts along dimension 0
- state_new_norm: float32 [2048], P(('job', 'replica')), parts along dimension 0
There are 2 independent parts, one for each index of `job`. A program takes and returns all parts, laid end to end along the dimension named above; each array names one. Nothing has to cross between parts.
All inputs are finite; a program needn't handle non-finite values.
Results may differ from a plain program's by a relative error of at most 0.0004.
Values may be sent and summed in bfloat16 or wider, within the bound.
A program may use at most 64 MiB of HBM per device.

v0:
```python
import jax
import jax.numpy as jnp
from jax import lax
from jax.sharding import PartitionSpec as P

learn_rate = 0.5
hold_rate = 0.9


def local(
    grad_query,
    grad_key,
    grad_value,
    grad_mixed,
    grad_norm,
    weight_query,
    weight_key,
    weight_value,
    weight_mixed,
    weight_norm,
    moment_query,
    moment_key,
    moment_value,
    moment_mixed,
    moment_norm,
):
    mean_query, mean_key, mean_value, mean_mixed = (
        lax.psum_scatter(grad_query[0], "replica", scatter_dimension=0, tiled=True),
        lax.psum_scatter(grad_key[0], "replica", scatter_dimension=0, tiled=True),
        lax.psum_scatter(grad_value[0], "replica", scatter_dimension=0, tiled=True),
        lax.psum_scatter(grad_mixed[0], "replica", scatter_dimension=1, tiled=True),
    )
    whole_norm = lax.psum(grad_norm[0], "replica")
    place = lax.axis_index("replica")
    mean_norm = lax.dynamic_slice_in_dim(
        whole_norm, place * weight_norm.shape[0], weight_norm.shape[0]
    )
    mean_rate = lax.axis_size("replica") ** (-0.5)
    mean_query = mean_query * mean_rate
    mean_key = mean_key * mean_rate
    mean_value = mean_value * mean_rate
    mean_mixed = mean_mixed * mean_rate
    mean_norm = mean_norm * mean_rate
    (
        own_query,
        own_key,
        own_value,
        own_mixed,
        slope_query_norm,
        slope_key_norm,
        slope_value_norm,
        slope_mixed_norm,
    ) = lax.psum(
        (
            jnp.sum(weight_query * weight_query, axis=1, keepdims=True),
            jnp.sum(weight_key * weight_key, axis=1, keepdims=True),
            jnp.sum(weight_value * weight_value, axis=1, keepdims=True),
            jnp.sum(weight_mixed * weight_mixed, axis=0, keepdims=True),
            jnp.sum(mean_query * mean_query, axis=1, keepdims=True),
            jnp.sum(mean_key * mean_key, axis=1, keepdims=True),
            jnp.sum(mean_value * mean_value, axis=1, keepdims=True),
            jnp.sum(mean_mixed * mean_mixed, axis=0, keepdims=True),
        ),
        "model",
    )
    mean_query = mean_query * (jnp.sqrt(own_query) * lax.rsqrt(slope_query_norm + 1e-06))
    mean_key = mean_key * (jnp.sqrt(own_key) * lax.rsqrt(slope_key_norm + 1e-06))
    mean_value = mean_value * (jnp.sqrt(own_value) * lax.rsqrt(slope_value_norm + 1e-06))
    mean_mixed = mean_mixed * (jnp.sqrt(own_mixed) * lax.rsqrt(slope_mixed_norm + 1e-06))
    state_new_query = hold_rate * moment_query + mean_query
    new_query = weight_query - learn_rate * state_new_query
    state_new_key = hold_rate * moment_key + mean_key
    new_key = weight_key - learn_rate * state_new_key
    state_new_value = hold_rate * moment_value + mean_value
    new_value = weight_value - learn_rate * state_new_value
    state_new_mixed = hold_rate * moment_mixed + mean_mixed
    new_mixed = weight_mixed - learn_rate * state_new_mixed
    state_new_norm = hold_rate * moment_norm + mean_norm
    new_norm = weight_norm - learn_rate * state_new_norm
    copy_query, copy_key, copy_value, copy_mixed, copy_norm = (
        lax.all_gather(new_query.astype(jnp.bfloat16), "replica", axis=0, tiled=True),
        lax.all_gather(new_key.astype(jnp.bfloat16), "replica", axis=0, tiled=True),
        lax.all_gather(new_value.astype(jnp.bfloat16), "replica", axis=0, tiled=True),
        lax.all_gather(new_mixed.astype(jnp.bfloat16), "replica", axis=1, tiled=True),
        lax.all_gather(new_norm.astype(jnp.bfloat16), "replica", axis=0, tiled=True),
    )
    return (
        copy_query,
        copy_key,
        copy_value,
        copy_mixed,
        copy_norm,
        new_query,
        new_key,
        new_value,
        new_mixed,
        new_norm,
        state_new_query,
        state_new_key,
        state_new_value,
        state_new_mixed,
        state_new_norm,
    )


def solution(mesh):
    placed = (
        P(("job", "replica"), None, "model"),
        P(("job", "replica"), None, "model"),
        P(("job", "replica"), None, "model"),
        P(("job", "replica"), "model", None),
        P(("job", "replica"), None),
        P(("job", "replica"), "model"),
        P(("job", "replica"), "model"),
        P(("job", "replica"), "model"),
        P(("job", "model"), "replica"),
        P(("job", "replica")),
        P(("job", "replica"), "model"),
        P(("job", "replica"), "model"),
        P(("job", "replica"), "model"),
        P(("job", "model"), "replica"),
        P(("job", "replica")),
    )
    return jax.shard_map(
        local,
        mesh=mesh,
        in_specs=placed,
        out_specs=(
            P("job", "model"),
            P("job", "model"),
            P("job", "model"),
            P(("job", "model"), None),
            P("job"),
            P(("job", "replica"), "model"),
            P(("job", "replica"), "model"),
            P(("job", "replica"), "model"),
            P(("job", "model"), "replica"),
            P(("job", "replica")),
            P(("job", "replica"), "model"),
            P(("job", "replica"), "model"),
            P(("job", "replica"), "model"),
            P(("job", "model"), "replica"),
            P(("job", "replica")),
        ),
        check_vma=False,
    )
```

profile of v0, /device:TPU:0, one launch (start us, length us, event | category | flops | bytes accessed | tf_op | source)
XLA Modules:
  0.0 210.1 jit_solution(8399502176376450542)
XLA Ops:
  10.1 13.5 %psum.71 = f32[1024]{0:T(1024)S(1)} all-reduce(f32[1024]{0:T(1024)S(1)} %bitcast.36), channel_id=1, replica_groups=mesh['job'=2,'replica'=4,'model'=4] {'replica'}, use_global_device_ids=true, to_apply=%region_20.0 | all-reduce | flops 1024 | bytes 8192 | tf_op jit(solution)/shard_map/psum | solution.py:33
  24.3 7.7 %all-gather = bf16[4,1,256]{2,1,0:T(2,128)(2,1)S(1)} all-gather(bf16[1,1,256]{2,1,0:T(2,128)(2,1)S(1)} %reshape.38), channel_id=1, replica_groups=mesh['job'=2,'replica'=4,'model'=4] {'replica'}, dimensions={0}, use_global_device_ids=true | all-gather | bytes 2560 | tf_op jit(solution)/shard_map/all_gather | solution.py:85
  32.8 0.8 copy-done
  33.8 6.6 %reduce-scatter.9.cloned.1.call-done = f32[256,256]{1,0:T(8,128)} async-done(((f32[1024,256]{1,0:T(8,128)}), f32[256,256]{1,0:T(8,128)}) %reduce-scatter.9.cloned.1.call-update) | async-done | bytes 262160 | tf_op jit(solution)/shard_map/reduce_scatter | solution.py:30
  40.4 1.1 multiply_reduce_fusion.2
  41.5 27.1 %reduce-scatter.11.cloned.1.call-done = f32[256,256]{1,0:T(8,128)} async-done(((f32[256,1024]{1,0:T(8,128)}), f32[256,256]{1,0:T(8,128)}) %reduce-scatter.11.cloned.1.call-update) | async-done | bytes 262160 | tf_op jit(solution)/shard_map/reduce_scatter | solution.py:31
  68.6 1.0 multiply_reduce_fusion
  69.6 27.1 %reduce-scatter.5.cloned.1.call-done = f32[256,256]{1,0:T(8,128)} async-done(((f32[1024,256]{1,0:T(8,128)}), f32[256,256]{1,0:T(8,128)}) %reduce-scatter.5.cloned.1.call-update) | async-done | bytes 262160 | tf_op jit(solution)/shard_map/reduce_scatter | solution.py:28
  96.7 1.1 multiply_reduce_fusion.6
  97.7 26.9 %reduce-scatter.7.cloned.1.call-done = f32[256,256]{1,0:T(8,128)} async-done(((f32[1024,256]{1,0:T(8,128)}), f32[256,256]{1,0:T(8,128)}) %reduce-scatter.7.cloned.1.call-update) | async-done | bytes 262160 | tf_op jit(solution)/shard_map/reduce_scatter | solution.py:29
  124.7 1.1 multiply_reduce_fusion.4
  125.8 10.0 %all-reduce = (f32[256,1]{0,1:T(1,128)S(1)}, f32[256,1]{0,1:T(1,128)S(1)}, f32[256,1]{0,1:T(1,128)S(1)}, f32[256,1]{0,1:T(1,128)S(1)}, f32[256,1]{0,1:T(1,128)S(...) all-reduce(f32[256,1]{0,1:T(1,128)S(1)} %bitcast.34, ...), channel_id=1, replica_groups=mesh['job'=2,'replica'=4,'model'=4] {'model'}, use_global_device_ids=true, to_apply=%region_4.0 | all-reduce | flops 2048 | bytes 16384 | tf_op jit(solution)/shard_map/psum | solution.py:53
  135.8 0.9 fusion.3
  136.7 14.8 %all_gather.16 = bf16[1024,256]{1,0:T(8,128)(2,1)S(1)} all-gather(bf16[256,256]{1,0:T(8,128)(2,1)S(1)} %get-tuple-element.32), channel_id=1, replica_groups=mesh['job'=2,'replica'=4,'model'=4] {'replica'}, dimensions={0}, use_global_device_ids=true | all-gather | bytes 655360 | tf_op jit(solution)/shard_map/all_gather | solution.py:82
  151.5 0.9 fusion.2
  152.4 15.3 %all_gather.17 = bf16[1024,256]{1,0:T(8,128)(2,1)S(1)} all-gather(bf16[256,256]{1,0:T(8,128)(2,1)S(1)} %get-tuple-element.29), channel_id=1, replica_groups=mesh['job'=2,'replica'=4,'model'=4] {'replica'}, dimensions={0}, use_global_device_ids=true | all-gather | bytes 655360 | tf_op jit(solution)/shard_map/all_gather | solution.py:83
  167.8 0.8 fusion.1
  168.6 16.1 %all_gather.18 = bf16[256,1024]{1,0:T(8,128)(2,1)S(1)} all-gather(bf16[256,256]{1,0:T(8,128)(2,1)S(1)} %get-tuple-element.26), channel_id=1, replica_groups=mesh['job'=2,'replica'=4,'model'=4] {'replica'}, dimensions={1}, use_global_device_ids=true | all-gather | bytes 655360 | tf_op jit(solution)/shard_map/all_gather | solution.py:84
  184.7 0.9 fusion.4
  185.7 14.8 %all_gather.15 = bf16[1024,256]{1,0:T(8,128)(2,1)S(1)} all-gather(bf16[256,256]{1,0:T(8,128)(2,1)S(1)} %get-tuple-element.35), channel_id=1, replica_groups=mesh['job'=2,'replica'=4,'model'=4] {'replica'}, dimensions={0}, use_global_device_ids=true | all-gather | bytes 655360 | tf_op jit(solution)/shard_map/all_gather | solution.py:81
  200.4 0.8 copy.35
  201.2 0.8 copy.36
  202.0 0.8 copy.37
  202.8 0.8 copy.38
  (48 shorter events, 4.6 us)
Async XLA Ops:
  7.2 33.2 %reduce-scatter.9.cloned.1.call-start = ((), (), s32[]{:S(2)}) async-start(), calls=%async_computation.6 | async-start | bytes 1310720 | tf_op jit(solution)/shard_map/reduce_scatter | solution.py:30
  7.9 60.6 %reduce-scatter.11.cloned.1.call-start = ((), (), s32[]{:S(2)}) async-start(), calls=%async_computation.7 | async-start | bytes 1310720 | tf_op jit(solution)/shard_map/reduce_scatter | solution.py:31
  8.7 88.0 %reduce-scatter.5.cloned.1.call-start = ((), (), s32[]{:S(2)}) async-start(), calls=%async_computation.4 | async-start | bytes 1310720 | tf_op jit(solution)/shard_map/reduce_scatter | solution.py:28
  9.4 115.2 %reduce-scatter.7.cloned.1.call-start = ((), (), s32[]{:S(2)}) async-start(), calls=%async_computation.5 | async-start | bytes 1310720 | tf_op jit(solution)/shard_map/reduce_scatter | solution.py:29
  9.4 0.7 copy-start.12
  9.5 14.1 %copy-start.13 = (f32[256]{0:T(256)S(1)}, f32[256]{0:T(256)}, u32[]{:S(2)}) copy-start(f32[256]{0:T(256)} %param.24) | copy-start | bytes 3076
  9.5 14.1 %copy-start.14 = (f32[256]{0:T(256)S(1)}, f32[256]{0:T(256)}, u32[]{:S(2)}) copy-start(f32[256]{0:T(256)} %param.29) | copy-start | bytes 3076
  9.5 23.1 %copy-start.3 = (f32[256,256]{1,0:T(8,128)S(1)}, f32[256,256]{1,0:T(8,128)}, u32[]{:S(2)}) copy-start(f32[256,256]{1,0:T(8,128)} %param.20) | copy-start | bytes 786436
  10.0 22.7 %copy-start.2 = (f32[256,256]{1,0:T(8,128)S(1)}, f32[256,256]{1,0:T(8,128)}, u32[]{:S(2)}) copy-start(f32[256,256]{1,0:T(8,128)} %param.23) | copy-start | bytes 786436
  32.6 1.0 copy-start
  32.7 1.0 copy-start.1
  69.6 66.2 %copy-start.8 = (f32[256,256]{1,0:T(8,128)S(1)}, f32[256,256]{1,0:T(8,128)}, u32[]{:S(2)}) copy-start(f32[256,256]{1,0:T(8,128)} %param.26) | copy-start | bytes 786436
  124.7 11.2 %copy-start.7 = (f32[256,256]{1,0:T(8,128)S(1)}, f32[256,256]{1,0:T(8,128)}, u32[]{:S(2)}) copy-start(f32[256,256]{1,0:T(8,128)} %reduce-scatter.7.cloned.1.call-done) | copy-start | bytes 786436
  136.7 14.8 %copy-start.6 = (f32[256,256]{1,0:T(8,128)S(1)}, f32[256,256]{1,0:T(8,128)}, u32[]{:S(2)}) copy-start(f32[256,256]{1,0:T(8,128)} %reduce-scatter.9.cloned.1.call-done) | copy-start | bytes 786436
  136.7 14.8 %copy-start.9 = (f32[256,256]{1,0:T(8,128)S(1)}, f32[256,256]{1,0:T(8,128)}, u32[]{:S(2)}) copy-start(f32[256,256]{1,0:T(8,128)} %param.27) | copy-start | bytes 786436
  152.4 15.3 %copy-start.5 = (f32[256,256]{1,0:T(8,128)S(1)}, f32[256,256]{1,0:T(8,128)}, u32[]{:S(2)}) copy-start(f32[256,256]{1,0:T(8,128)} %reduce-scatter.11.cloned.1.call-done) | copy-start | bytes 786436
  152.4 15.4 %copy-start.10 = (f32[256,256]{1,0:T(8,128)S(1)}, f32[256,256]{1,0:T(8,128)}, u32[]{:S(2)}) copy-start(f32[256,256]{1,0:T(8,128)} %param.28) | copy-start | bytes 786436
  168.6 16.1 %copy-start.4 = (f32[256,256]{1,0:T(8,128)S(1)}, f32[256,256]{1,0:T(8,128)}, u32[]{:S(2)}) copy-start(f32[256,256]{1,0:T(8,128)} %reduce-scatter.5.cloned.1.call-done) | copy-start | bytes 786436
  168.6 16.1 %copy-start.11 = (f32[256,256]{1,0:T(8,128)S(1)}, f32[256,256]{1,0:T(8,128)}, u32[]{:S(2)}) copy-start(f32[256,256]{1,0:T(8,128)} %param.25) | copy-start | bytes 786436
Sparse Core Ops, SparseCore 0:
  10.3 30.1 reduce-scatter.8
  42.7 25.7 reduce-scatter.10
  70.9 25.7 reduce-scatter.4
  98.8 25.7 reduce-scatter.6
where the time goes:
time: 210 us
  blocking collectives  92.1 us (44%)
  waiting for transfers between devices  90.2 us (43%)
  between operations  14 us (7%)
  other arithmetic  8.91 us (4%)
  local copies, waits for them, and re-layouts  4.75 us (2%)
    reduce_scatter x1, waiting for transfers between devices, local(): lax.psum_scatter(grad_query[0], 'replica', scatter_dimension=0, tiled=True)  27.1 us
    reduce_scatter x1, waiting for transfers between devices, local(): lax.psum_scatter(grad_mixed[0], 'replica', scatter_dimension=1, tiled=True)  27.1 us
    reduce_scatter x1, waiting for transfers between devices, local(): lax.psum_scatter(grad_key[0], 'replica', scatter_dimension=0, tiled=True)  26.9 us
    all_gather x1, blocking collectives, local(): lax.all_gather(new_mixed.astype(jnp.bfloat16), 'replica', axis=1, tiled=T...  16.1 us
    all_gather x1, blocking collectives, local(): lax.all_gather(new_value.astype(jnp.bfloat16), 'replica', axis=0, tiled=T...  15.3 us
    all_gather x1, blocking collectives, local(): lax.all_gather(new_key.astype(jnp.bfloat16), 'replica', axis=0, tiled=True)  14.8 us
    all_gather x1, blocking collectives, local(): lax.all_gather(new_query.astype(jnp.bfloat16), 'replica', axis=0, tiled=T...  14.8 us
    psum x1, blocking collectives, local(): whole_norm = lax.psum(grad_norm[0], 'replica')  13.5 us
  transfers between devices with their start and end apart: 4, of which 4 were waited for; matrix products, arithmetic and copies ran while one was open for 2% of the time, Pallas kernels for 0%

commit v1 on v0

--- a/solution.py
+++ b/solution.py
@@ -1,6 +1,10 @@
+import functools
+
 import jax
 import jax.numpy as jnp
 from jax import lax
+from jax.experimental import pallas as pl
+from jax.experimental.pallas import tpu as pltpu
 from jax.sharding import PartitionSpec as P
 
 learn_rate = 0.5
@@ -103,6 +107,332 @@
     )
 
 
+MESH = pl.DeviceIdType.MESH
+EPS = 1e-06
+SPAN = 228.0
+FLOOR = 2.0 ** (-125 / 32)
+
+
+def encode(x, scale):
+    b = jnp.abs(x) * ((SPAN * FLOOR) / scale) + FLOOR
+    for _ in range(5):
+        b = b * b
+    return jnp.where(x < 0.0, -b, b).astype(jnp.bfloat16)
+
+
+def decode(y, scale):
+    y = y.astype(jnp.float32)
+    r = jnp.abs(y)
+    for _ in range(4):
+        r = lax.rsqrt(r)
+    u = (r * lax.rsqrt(r) - FLOOR) * (scale * (1.0 / (SPAN * FLOOR)))
+    return jnp.where(y < 0.0, -u, u)
+
+
+def kernel(n, nm, mats, *refs):
+    k = len(mats)
+    refs = list(refs)
+
+    def take(count):
+        out = refs[:count]
+        del refs[:count]
+        return out
+
+    grads, (gnorm_in,) = take(k), take(1)
+    weights, (wnorm_in,) = take(k), take(1)
+    moments, (mnorm_in,) = take(k), take(1)
+    copies, (copy_norm,) = take(k), take(1)
+    news, (new_norm,) = take(k), take(1)
+    states, (state_norm,) = take(k), take(1)
+    G, W, M, enc, got, total, stat, statg, ng, nw, nmo = take(11)
+    gsem, wsem, msem, rs_s, rs_r, ag_s, ag_r, st_s, st_r, no_s, no_r = take(11)
+
+    rows, cols = W.shape[1], W.shape[2]
+    block = 64
+    me = lax.axis_index("replica")
+    mm = lax.axis_index("model")
+    rate = n ** (-0.5)
+
+    def part(ref, m, t):
+        if mats[m] == 0:
+            return ref.at[pl.ds(pl.multiple_of(t * rows, rows), rows), :]
+        return ref.at[:, pl.ds(pl.multiple_of(t * cols, cols), cols)]
+
+    def g_copy(m, t):
+        return pltpu.make_async_copy(part(grads[m].at[0], m, t), G.at[m, t], gsem.at[m, t])
+
+    def w_copy(m):
+        return pltpu.make_async_copy(weights[m], W.at[m], wsem.at[m])
+
+    def m_copy(m):
+        return pltpu.make_async_copy(moments[m], M.at[m], msem.at[m])
+
+    barrier = pltpu.get_barrier_semaphore()
+    for d in range(1, n):
+        pl.semaphore_signal(barrier, 1, device_id={"replica": lax.rem(me + d, n)}, device_id_type=MESH)
+    for d in range(1, nm):
+        pl.semaphore_signal(barrier, 1, device_id={"model": lax.rem(mm + d, nm)}, device_id_type=MESH)
+    for m in range(k):
+        for t in range(n):
+            g_copy(m, t).start()
+        w_copy(m).start()
+        m_copy(m).start()
+
+    near = jnp.where(2 * me < n, 0, 1)
+
+    def mirror(direction, i):
+        return jnp.where(direction == 0, i, n - 1 - i)
+
+    def rs_copy(direction, m, t, to):
+        return pltpu.make_async_remote_copy(
+            src_ref=enc.at[direction, m, t], dst_ref=got.at[direction, m, t],
+            send_sem=rs_s.at[direction, m, t], recv_sem=rs_r.at[direction, m, t],
+            device_id={"replica": to}, device_id_type=MESH)
+
+    def neighbour(direction):
+        return jnp.clip(jnp.where(direction == 0, me + 1, me - 1), 0, n - 1)
+
+    def blocks(body):
+        @pl.loop(0, rows // block)
+        def _(i):
+            body(pl.ds(pl.multiple_of(i * block, block), block))
+
+    def scale_of(direction, m, t):
+        return got[direction, m, t, rows:rows + 8, :].astype(jnp.float32)[0:1]
+
+    def rs_step(m, direction, s):
+        place = mirror(direction, me)
+        t = mirror(direction, n - 1 - s)
+
+        @pl.when((n - 1 - s > place) & (place > 0))
+        def _():
+            rs_copy(direction, m, t, neighbour(direction)).wait_recv()
+            scale = scale_of(direction, m, t)
+
+            def body(r):
+                G[m, t, r, :] = G[m, t, r, :] + decode(got[direction, m, t, r, :], scale)
+            blocks(body)
+
+        @pl.when(n - 1 - s > place)
+        def _():
+            def largest(i, top):
+                x = jnp.abs(G[m, t, pl.ds(pl.multiple_of(i * block, block), block), :])
+                return jnp.maximum(top, jnp.max(x.reshape(block // 8, 8, cols), axis=0))
+
+            top = lax.fori_loop(0, rows // block, largest, jnp.zeros((8, cols), jnp.float32))
+            top = jnp.max(top, axis=0, keepdims=True) * 1.0079 + 1e-30
+            top = jnp.broadcast_to(top, (8, cols)).astype(jnp.bfloat16)
+            enc[direction, m, t, rows:rows + 8, :] = top
+            scale = top.astype(jnp.float32)[0:1]
+
+            def body(r):
+                enc[direction, m, t, r, :] = encode(G[m, t, r, :], scale)
+            blocks(body)
+            rs_copy(direction, m, t, neighbour(direction)).start()
+
+    def stat_copy(m, d):
+        peer = lax.rem(mm + d, nm)
+        return pltpu.make_async_remote_copy(
+            src_ref=stat.at[m], dst_ref=statg.at[m, d - 1], send_sem=st_s.at[m, d - 1], recv_sem=st_r.at[m, d - 1],
+            device_id={"model": peer}, device_id_type=MESH)
+
+    def squares(x, dim):
+        x = x * x
+        if dim == 1:
+            return jnp.sum(x, axis=0, keepdims=True)
+        half = functools.reduce(jnp.add, [x[:, c:c + 128] for c in range(0, cols, 128)])
+        return jnp.sum(half.T, axis=0, keepdims=True)
+
+    def own_stat(m):
+        w_copy(m).wait()
+        stat[m, 0:1, :] = squares(W[m], mats[m])
+
+    def total_of(m):
+        for direction in range(2):
+            @pl.when(mirror(direction, me) > 0)
+            def _():
+                rs_copy(direction, m, me, neighbour(direction)).wait_recv()
+
+        def add(*directions):
+            scales = {d: scale_of(d, m, me) for d in directions}
+
+            def body(r):
+                u = functools.reduce(jnp.add, [decode(got[d, m, me, r, :], scales[d]) for d in directions])
+                total[m, r, :] = (G[m, me, r, :] + u) * rate
+            blocks(body)
+
+        pl.when(me == 0)(lambda: add(1))
+        pl.when(me == n - 1)(lambda: add(0))
+        pl.when((me > 0) & (me < n - 1))(lambda: add(0, 1))
+        stat[m, 1:2, :] = squares(total[m], mats[m])
+        for d in range(1, nm):
+            stat_copy(m, d).start()
+
+    def ag_copy(direction, m, t):
+        piece = part(copies[m], m, t)
+        return pltpu.make_async_remote_copy(
+            src_ref=piece, dst_ref=piece, send_sem=ag_s.at[direction, m, t], recv_sem=ag_r.at[direction, m, t],
+            device_id={"replica": neighbour(direction)}, device_id_type=MESH)
+
+    def update(m):
+        for d in range(1, nm):
+            stat_copy(m, d).wait_recv()
+        sums = stat[m]
+        for d in range(nm - 1):
+            sums = sums + statg[m, d]
+        ratio = jnp.sqrt(sums[0:1]) * lax.rsqrt(sums[1:2] + EPS)
+        if mats[m] == 0:
+            turned = jnp.broadcast_to(ratio, (128, rows)).T
+            ratio = jnp.concatenate([turned] * (cols // 128), axis=1)
+        m_copy(m).wait()
+        state = hold_rate * M[m] + total[m] * ratio
+        new = W[m] - learn_rate * state
+        states[m][...] = state
+        news[m][...] = new
+        part(copies[m], m, me)[...] = new.astype(jnp.bfloat16)
+        for direction in range(2):
+            @pl.when(mirror(direction, me) < n - 1)
+            def _():
+                ag_copy(direction, m, me).start()
+
+    def relay(m, direction, s):
+        place = mirror(direction, me)
+        t = mirror(direction, jnp.maximum(place - 1 - s, 0))
+
+        @pl.when(place - 1 - s >= 0)
+        def _():
+            ag_copy(direction, m, t).wait_recv()
+
+        @pl.when((place - 1 - s >= 0) & (place < n - 1))
+        def _():
+            ag_copy(direction, m, t).start()
+
+    def norm_copies(d):
+        to = lax.rem(me + d, n)
+        return [pltpu.make_async_remote_copy(
+            src_ref=src, dst_ref=dst.at[me], send_sem=no_s.at[i, d - 1], recv_sem=no_r.at[i, d - 1],
+            device_id={"replica": to}, device_id_type=MESH)
+            for i, (src, dst) in enumerate(((gnorm_in, ng), (wnorm_in, nw), (mnorm_in, nmo)))]
+
+    def reduce_scatter(m):
+        for t in range(n):
+            g_copy(m, t).wait()
+        for s in range(n - 1):
+            rs_step(m, near, s)
+            rs_step(m, 1 - near, s)
+
+    pl.semaphore_wait(barrier, n - 1 + nm - 1)
+    for m in range(k):
+        reduce_scatter(m)
+        if m == 0:
+            for d in range(1, n):
+                for c in norm_copies(d):
+                    c.start()
+            ng[me] = gnorm_in[...]
+            nw[me] = wnorm_in[...]
+            nmo[me] = mnorm_in[...]
+        own_stat(m)
+        total_of(m)
+        if m >= 1:
+            update(m - 1)
+        if m >= 2:
+            for s in range(n - 1):
+                for direction in range(2):
+                    relay(m - 2, direction, s)
+    update(k - 1)
+    for d in range(1, n):
+        for c in norm_copies(d):
+            c.wait_recv()
+    width = wnorm_in.shape[1]
+    mean = functools.reduce(jnp.add, [ng[t] for t in range(n)]) * rate
+    for t in range(n):
+        state = hold_rate * nmo[t] + mean[:, t * width:(t + 1) * width]
+        new = nw[t] - learn_rate * state
+        copy_norm[:, t * width:(t + 1) * width] = new.astype(jnp.bfloat16)
+
+        @pl.when(me == t)
+        def _():
+            state_norm[...] = state
+            new_norm[...] = new
+    for m in range(max(k - 2, 0), k):
+        for s in range(n - 1):
+            for direction in range(2):
+                relay(m, direction, s)
+    for d in range(1, n):
+        for c in norm_copies(d):
+            c.wait_send()
+    for m in range(k):
+        for d in range(1, nm):
+            stat_copy(m, d).wait_send()
+        for direction in range(2):
+            place = mirror(direction, me)
+            for s in range(n):
+                t = mirror(direction, n - 1 - s)
+
+                @pl.when(n - 1 - s > place)
+                def _():
+                    rs_copy(direction, m, t, neighbour(direction)).wait_send()
+
+                @pl.when((n - 1 - s <= place) & (place < n - 1))
+                def _():
+                    ag_copy(direction, m, t).wait_send()
+
+
+def fused(n, nm, *args):
+    k = 4
+    grads, weights, moments = args[:k], args[k + 1:2 * k + 1], args[2 * k + 2:3 * k + 2]
+    gnorm, wnorm, mnorm = args[k], args[2 * k + 1], args[3 * k + 2]
+    mats = tuple(0 if g.shape[1] != w.shape[0] else 1 for g, w in zip(grads, weights))
+    rows, cols = weights[0].shape
+    f32, b16 = jnp.float32, jnp.bfloat16
+    width = wnorm.shape[0]
+    any_, vmem = pl.BlockSpec(memory_space=pl.ANY), pl.BlockSpec(memory_space=pltpu.VMEM)
+    shape = jax.ShapeDtypeStruct
+    out_shape = (
+        [shape(g.shape[1:], b16) for g in grads] + [shape((1, n * width), b16)]
+        + [shape((rows, cols), f32)] * k + [shape((1, width), f32)]
+        + [shape((rows, cols), f32)] * k + [shape((1, width), f32)]
+    )
+    dma = pltpu.SemaphoreType.DMA
+    outs = pl.pallas_call(
+        functools.partial(kernel, n, nm, mats),
+        out_shape=out_shape,
+        in_specs=([any_] * k + [vmem]) * 3,
+        out_specs=[vmem] * len(out_shape),
+        scratch_shapes=[
+            pltpu.VMEM((k, n, rows, cols), f32),
+            pltpu.VMEM((k, rows, cols), f32),
+            pltpu.VMEM((k, rows, cols), f32),
+            pltpu.VMEM((2, k, n, rows + 8, cols), b16),
+            pltpu.VMEM((2, k, n, rows + 8, cols), b16),
+            pltpu.VMEM((k, rows, cols), f32),
+            pltpu.VMEM((k, 2, cols), f32),
+            pltpu.VMEM((k, nm - 1, 2, cols), f32),
+            pltpu.VMEM((n, 1, n * width), f32),
+            pltpu.VMEM((n, 1, width), f32),
+            pltpu.VMEM((n, 1, width), f32),
+            dma((k, n)), dma((k,)), dma((k,)),
+            dma((2, k, n)), dma((2, k, n)), dma((2, k, n)), dma((2, k, n)),
+            dma((k, nm - 1)), dma((k, nm - 1)), dma((3, n - 1)), dma((3, n - 1)),
+        ],
+        compiler_params=pltpu.CompilerParams(
+            collective_id=0, has_side_effects=True, vmem_limit_bytes=48 * 2**20
+        ),
+    )(*grads, gnorm, *weights, wnorm.reshape(1, width), *moments, mnorm.reshape(1, width))
+    outs = list(outs)
+    for i in range(k, len(outs), k + 1):
+        outs[i] = outs[i].reshape(-1)
+    return tuple(outs)
+
+
+def pick(n, nm, *args):
+    weights = args[5:9]
+    fits = all(w.shape == weights[0].shape and w.shape[0] == w.shape[1] and w.shape[0] % 128 == 0 for w in weights)
+    if 1 < n <= 4 and nm > 1 and fits and args[9].shape[0] % 128 == 0:
+        return fused(n, nm, *args)
+    return local(*args)
+
+
 def solution(mesh):
     placed = (
         P(("job", "replica"), None, "model"),
@@ -122,7 +452,7 @@
         P(("job", "replica")),
     )
     return jax.shard_map(
-        local,
+        functools.partial(pick, mesh.shape["replica"], mesh.shape["model"]),
         mesh=mesh,
         in_specs=placed,
         out_specs=(

time: 210 us -> 124 us (0.59)
  Pallas kernels: 0 us -> 102 us
  blocking collectives: 92.1 us -> 0 us
  waiting for transfers between devices: 90.2 us -> 0 us
  local copies, waits for them, and re-layouts: 4.75 us -> 20.3 us
  between operations: 14 us -> 0.7 us
  other arithmetic: 8.91 us -> 0.6 us
    pallas_call x0 -> x1, Pallas kernels: none -> 102 us  [fused(): pl.pallas_call(functools.partial(kernel, n, nm, mats), out_shape=out_shap...]
    reduce_scatter x4 -> x0, waiting for transfers between devices: 87.7 us -> none  [the longest x1 27.1 us: local(): lax.psum_scatter(grad_query[0], 'replica', scatter_dimension=0, tiled=True)]
    all_gather x5 -> x0, blocking collectives: 68.7 us -> none  [the longest x1 16.1 us: local(): lax.all_gather(new_mixed.astype(jnp.bfloat16), 'replica', axis=1, tiled=T...]
    psum x2 -> x0, blocking collectives: 23.4 us -> none  [the longest x1 13.5 us: local(): whole_norm = lax.psum(grad_norm[0], 'replica')]
    unnamed x36 -> x42, local copies, waits for them, and re-layouts: 4.75 us -> 20.3 us
    reduce_sum x8 -> x0, other arithmetic: 4.64 us -> none  [the longest x1 1.13 us: local(): jnp.sum(mean_key * mean_key, axis=1, keepdims=True)]
    convert_element_type x5 -> x0, other arithmetic: 4.21 us -> none  [the longest x1 0.91 us: local(): new_query.astype(jnp.bfloat16)]
    unnamed x4 -> x0, waiting for transfers between devices: 2.54 us -> none
  transfers between devices with their start and end apart: 4 -> 0, of which waited for: 4 -> 0; matrix products, arithmetic and copies ran while one was open for 2% -> 0% of each run, Pallas kernels for 0% -> 0%
where the time goes in v1:
time: 124 us
  Pallas kernels  102 us (82%)
  local copies, waits for them, and re-layouts  20.3 us (16%)
    pallas_call x1, Pallas kernels, fused(): pl.pallas_call(functools.partial(kernel, n, nm, mats), out_shape=out_shap...  102 us
    unnamed x42, local copies, waits for them, and re-layouts  20.3 us

profile of v1, /device:TPU:0, one launch (start us, length us, event | category | flops | bytes accessed | tf_op | source)
XLA Modules:
  0.0 123.8 jit_solution(11957106808315853789)
XLA Ops:
  0.7 0.7 copy-done.12
  1.4 0.9 copy-done
  2.3 0.9 copy-done.1
  3.3 0.9 copy-done.2
  4.2 0.9 copy-done.3
  5.2 0.9 copy-done.4
  6.1 0.9 copy-done.5
  7.1 0.9 copy-done.6
  8.0 0.9 copy-done.7
  9.0 0.7 copy-done.10
  9.6 102.2 %shard_map.262 = (bf16[1024,256]{1,0:T(8,128)(2,1)S(1)}, bf16[1024,256]{1,0:T(8,128)(2,1)S(1)}, bf16[1024,256]{1,0:T(8,128)(2,1)S(1)}, bf16[256,1024]{1,0:T(8,12...) custom-call(f32[1,1024,256]{2,1,0:T(8,128)} %refs_0_.1, ...), custom_call_target="tpu_custom_call" | custom-call | tf_op jit(solution)/shard_map/pallas_call | solution.py:397
  111.9 0.7 copy-done.8
  113.2 0.8 copy.44
  114.0 0.8 copy.45
  114.8 0.8 copy.46
  116.0 0.8 copy.47
  117.1 0.7 copy.48
  117.8 0.7 copy.49
  118.5 0.7 copy.50
  119.2 0.7 copy.51
  120.4 0.7 copy.53
  121.2 0.7 copy.54
  121.9 0.7 copy.55
  122.6 0.7 copy.56
  (20 shorter events, 2.5 us)
Async XLA Ops:
  0.7 0.7 copy-start.12
  0.7 0.7 copy-start.11
  1.3 0.9 copy-start
  2.3 0.9 copy-start.1
  3.2 0.9 copy-start.2
  4.2 0.9 copy-start.3
  5.2 0.9 copy-start.4
  6.1 0.9 copy-start.5
  7.1 0.9 copy-start.6
  8.0 0.9 copy-start.7
  9.0 0.7 copy-start.10
  111.9 0.7 copy-start.8
  114.8 1.2 copy-start.13
  116.0 1.1 copy-start.9

commit v2 on v1

--- a/solution.py
+++ b/solution.py
@@ -322,24 +322,29 @@
             rs_step(m, 1 - near, s)
 
     pl.semaphore_wait(barrier, n - 1 + nm - 1)
-    for m in range(k):
-        reduce_scatter(m)
-        if m == 0:
+    def relays(m):
+        for s in range(n - 1):
+            for direction in range(2):
+                relay(m, direction, s)
+
+    for i in range(k + 3):
+        if i < k:
+            reduce_scatter(i)
+        if i == 0:
             for d in range(1, n):
                 for c in norm_copies(d):
                     c.start()
             ng[me] = gnorm_in[...]
             nw[me] = wnorm_in[...]
             nmo[me] = mnorm_in[...]
-        own_stat(m)
-        total_of(m)
-        if m >= 1:
-            update(m - 1)
-        if m >= 2:
-            for s in range(n - 1):
-                for direction in range(2):
-                    relay(m - 2, direction, s)
-    update(k - 1)
+        if i < k:
+            own_stat(i)
+        if 0 <= i - 2 < k:
+            update(i - 2)
+        if 0 <= i - 1 < k:
+            total_of(i - 1)
+        if 0 <= i - 3 < k - 2:
+            relays(i - 3)
     for d in range(1, n):
         for c in norm_copies(d):
             c.wait_recv()
@@ -354,10 +359,8 @@
         def _():
             state_norm[...] = state
             new_norm[...] = new
-    for m in range(max(k - 2, 0), k):
-        for s in range(n - 1):
-            for direction in range(2):
-                relay(m, direction, s)
+    for m in range(k - 2, k):
+        relays(m)
     for d in range(1, n):
         for c in norm_copies(d):
             c.wait_send()
@@ -386,7 +389,7 @@
     rows, cols = weights[0].shape
     f32, b16 = jnp.float32, jnp.bfloat16
     width = wnorm.shape[0]
-    any_, vmem = pl.BlockSpec(memory_space=pl.ANY), pl.BlockSpec(memory_space=pltpu.VMEM)
+    any_, vmem = pl.BlockSpec(memory_space=pltpu.HBM), pl.BlockSpec(memory_space=pltpu.VMEM)
     shape = jax.ShapeDtypeStruct
     out_shape = (
         [shape(g.shape[1:], b16) for g in grads] + [shape((1, n * width), b16)]

time: 124 us -> 105 us (0.85)
  Pallas kernels: 102 us -> 83.1 us
    pallas_call x1, Pallas kernels: 102 us -> 83.1 us  [fused(): pl.pallas_call(functools.partial(kernel, n, nm, mats), out_shape=out_shap...]
where the time goes in v2:
time: 105 us
  Pallas kernels  83.1 us (79%)
  local copies, waits for them, and re-layouts  20.3 us (19%)
    pallas_call x1, Pallas kernels, fused(): pl.pallas_call(functools.partial(kernel, n, nm, mats), out_shape=out_shap...  83.1 us
    unnamed x42, local copies, waits for them, and re-layouts  20.3 us

profile of v2, /device:TPU:0, one launch (start us, length us, event | category | flops | bytes accessed | tf_op | source)
XLA Modules:
  0.0 104.7 jit_solution(1031609858417670739)
XLA Ops:
  0.7 0.7 copy-done.12
  1.4 0.9 copy-done
  2.3 0.9 copy-done.1
  3.3 0.9 copy-done.2
  4.2 0.9 copy-done.3
  5.2 0.9 copy-done.4
  6.1 0.9 copy-done.5
  7.1 0.9 copy-done.6
  8.0 0.9 copy-done.7
  9.0 0.7 copy-done.10
  9.6 83.1 %shard_map.262 = (bf16[1024,256]{1,0:T(8,128)(2,1)S(1)}, bf16[1024,256]{1,0:T(8,128)(2,1)S(1)}, bf16[1024,256]{1,0:T(8,128)(2,1)S(1)}, bf16[256,1024]{1,0:T(8,12...) custom-call(f32[1,1024,256]{2,1,0:T(8,128)} %refs_0_.1, ...), custom_call_target="tpu_custom_call" | custom-call | tf_op jit(solution)/shard_map/pallas_call | solution.py:400
  92.8 0.7 copy-done.8
  94.1 0.8 copy.44
  94.9 0.8 copy.45
  95.7 0.8 copy.46
  96.9 0.8 copy.47
  98.0 0.7 copy.48
  98.7 0.7 copy.49
  99.4 0.7 copy.50
  100.1 0.7 copy.51
  101.3 0.7 copy.53
  102.1 0.7 copy.54
  102.8 0.7 copy.55
  103.5 0.7 copy.56
  (20 shorter events, 2.5 us)
Async XLA Ops:
  0.7 0.7 copy-start.12
  0.7 0.7 copy-start.11
  1.3 0.9 copy-start
  2.3 0.9 copy-start.1
  3.2 0.9 copy-start.2
  4.2 0.9 copy-start.3
  5.2 0.9 copy-start.4
  6.1 0.9 copy-start.5
  7.1 0.9 copy-start.6
  8.0 0.9 copy-start.7
  9.0 0.7 copy-start.10
  92.8 0.7 copy-start.8
  95.7 1.2 %copy-start.13 = (bf16[256,1024]{1,0:T(8,128)(2,1)S(1)}, bf16[256,1024]{1,0:T(8,128)(2,1)}, u32[]{:S(2)}) copy-start(bf16[256,1024]{1,0:T(8,128)(2,1)} %get-tuple-element.63) | copy-start | bytes 1572868
  96.9 1.1 %copy-start.9 = (f32[256,256]{1,0:T(8,128)S(1)}, f32[256,256]{1,0:T(8,128)}, u32[]{:S(2)}) copy-start(f32[256,256]{1,0:T(8,128)} %copy-done.8) | copy-start | bytes 786436
